TPU v7x, 128 devices: a whole 4x4x4 slice. The times are simulated.
128 devices in a mesh: rows: 4 (over z), cols: 8 (over x, core), slabs: 4 (over y).
Axes of the slice: x: 4, y: 4, z: 4, core: 2. Of those that a mesh axis runs over, the one named last changes fastest.
Arguments:
- pressure: float32 [512, 32, 128, 128], P('rows', 'cols', 'slabs'), may hold values from 0.5 to 2
- earlier: float32 [512, 32, 128, 128], P('rows', 'cols', 'slabs'), may hold values from 0.2 to 1.8
- speed_square: float32 [512, 32, 128, 128], P('rows', 'cols', 'slabs'), may hold values from 0.05 to 0.3
Outputs:
- scaled_field: float32 [512, 32, 128, 128], P('rows', 'cols', 'slabs')
- pressure_end: float32 [512, 32, 128, 128], P('rows', 'cols', 'slabs')
All inputs are finite; a program needn't handle non-finite values.
Results may differ from a plain program's by a relative error of at most 0.00002.
Values sent between devices are 32-bit elements; how exact they have to be, the bound alone decides.
A program may use at most 128 MiB of HBM per device.

v0:
```python
import functools

import jax
import jax.numpy as jnp
from jax import lax
from jax.experimental import pallas as pl
from jax.experimental.pallas import tpu as pltpu
from jax.sharding import PartitionSpec as P

STEPS = 3
MESH = pl.DeviceIdType.MESH
T = 8
ORDER = (3, 0, 1, 2)
GUESS = 1.0
UNROLL = 2


def exchange_kernel(
    p_hbm, e_hbm, s_hbm, out, norm,
    a, b, s, stats,
    load_sem, far_send, far_recv, near_send, near_recv,
    z_send, z_recv, y_send, y_recv, st_send, st_recv,
):
    nj, ni, nk, _ = out.shape
    tiles = nk // T
    zs, ys, xs = (lax.axis_size("rows"), lax.axis_size("slabs"), lax.axis_size("cols"))
    z, y, x = (lax.axis_index("rows"), lax.axis_index("slabs"), lax.axis_index("cols"))
    core = x % 2
    far_x = (x + 2 * core - 1 + xs) % xs
    near_x = x + 1 - 2 * core
    far, near = (1 + (ni - 1) * core, ni - (ni - 1) * core)
    far_halo, near_halo = ((ni + 1) * core, (ni + 1) * (1 - core))
    z_up, z_down = ((z + 1) % zs, (z + zs - 1) % zs)
    y_up, y_down = ((y + 1) % ys, (y + ys - 1) % ys)
    body = pl.ds(1, nj)
    levels = (a, b, a)

    def local(src, dst, n):
        return pltpu.make_async_copy(src, dst, load_sem.at[n])

    def rows_of(kc):
        return pl.ds(T + kc * T, T)

    loads = {}
    for n, kc in enumerate(ORDER):
        loads["far", kc] = local(
            p_hbm.at[:, far - 1, pl.ds(kc * T, T), :], a.at[body, far, rows_of(kc), :], n
        )
    n = tiles
    loads["near"] = local(p_hbm.at[:, near - 1], a.at[body, near, pl.ds(T, nk), :], n)
    loads["mid"] = local(p_hbm.at[:, pl.ds(1, ni - 2)], a.at[body, pl.ds(2, ni - 2), pl.ds(T, nk), :], n + 1)
    n += 2
    for kc in ORDER:
        loads["e", kc] = local(
            e_hbm.at[:, :, pl.ds(kc * T, T), :], b.at[body, pl.ds(1, ni), rows_of(kc), :], n
        )
        loads["s", kc] = local(
            s_hbm.at[:, :, pl.ds(kc * T, T), :], s.at[:, :, pl.ds(kc * T, T), :], n + 1
        )
        n += 2
    for copy in loads.values():
        copy.start()

    def remote(src, dst, send, recv, **where):
        return pltpu.make_async_remote_copy(
            src_ref=src, dst_ref=dst, send_sem=send, recv_sem=recv, device_id=where, device_id_type=MESH
        )

    def far_copy(t, kc):
        ref = levels[t]
        return remote(
            ref.at[body, far, rows_of(kc), :],
            ref.at[body, (ni + 1) * (1 - core), rows_of(kc), :],
            far_send.at[t, kc], far_recv.at[t, kc], cols=far_x,
        )

    def near_copy(t, kc):
        ref = levels[t]
        return remote(
            ref.at[body, near, rows_of(kc), :],
            ref.at[body, (ni + 1) * core, rows_of(kc), :],
            near_send.at[t, kc], near_recv.at[t, kc], cols=near_x,
        )

    def z_copies(t, kc):
        ref = levels[t]
        cells = pl.ds(1, ni)
        return (
            remote(
                ref.at[nj, cells, rows_of(kc), :], ref.at[0, cells, rows_of(kc), :],
                z_send.at[0, t, kc], z_recv.at[0, t, kc], rows=z_up,
            ),
            remote(
                ref.at[1, cells, rows_of(kc), :], ref.at[nj + 1, cells, rows_of(kc), :],
                z_send.at[1, t, kc], z_recv.at[1, t, kc], rows=z_down,
            ),
        )

    def y_copy(t, kc):
        ref = levels[t]
        cells = pl.ds(1, ni)
        if kc == 0:
            return remote(
                ref.at[body, cells, pl.ds(T, 1), :], ref.at[body, cells, pl.ds(T + nk, 1), :],
                y_send.at[0, t], y_recv.at[0, t], slabs=y_down,
            )
        return remote(
            ref.at[body, cells, pl.ds(T + nk - 1, 1), :], ref.at[body, cells, pl.ds(T - 1, 1), :],
            y_send.at[1, t], y_recv.at[1, t], slabs=y_up,
        )

    def faces(t, kc):
        yield far_copy(t, kc)
        yield near_copy(t, kc)
        yield from z_copies(t, kc)
        if kc in (0, tiles - 1):
            yield y_copy(t, kc)

    def wait_around(t, kc):
        near_copy(t, kc).wait_recv()
        for copy in z_copies(t, kc):
            copy.wait_recv()
        if kc == 0:
            y_copy(t, tiles - 1).wait_recv()
        if kc == tiles - 1:
            y_copy(t, 0).wait_recv()

    def stepped(now, before, j, i, kc):
        r = T + kc * T
        middle = now[j, i, pl.ds(r, T), :]
        total = now[j - 1, i, pl.ds(r, T), :] + now[j + 1, i, pl.ds(r, T), :]
        total = total + now[j, i - 1, pl.ds(r, T), :] + now[j, i + 1, pl.ds(r, T), :]
        total = total + now[j, i, pl.ds(r - 1, T), :] + now[j, i, pl.ds(r + 1, T), :]
        spread = total - 6.0 * middle
        earlier = before[j, i, pl.ds(r, T), :]
        return 2.0 * middle - earlier + s[j - 1, i - 1, pl.ds(kc * T, T), :] * spread

    barrier = pltpu.get_barrier_semaphore()
    peers = [dict(cols=far_x), dict(cols=near_x), dict(slabs=y_up), dict(slabs=y_down)]
    others = [dict(rows=(z + d) % zs) for d in range(1, zs)]
    for where in peers + others:
        pl.semaphore_signal(barrier, inc=1, device_id=where, device_id_type=MESH)
    pl.semaphore_wait(barrier, len(peers) + len(others))

    for kc in ORDER:
        loads["far", kc].wait()
        far_copy(0, kc).start()
    loads["near"].wait()
    for kc in ORDER:
        near_copy(0, kc).start()
    loads["mid"].wait()
    for kc in ORDER:
        for copy in z_copies(0, kc):
            copy.start()
    y_copy(0, tiles - 1).start()
    y_copy(0, 0).start()

    for t in range(STEPS - 1):
        now, before = (levels[t], levels[(t + 1) % 2])
        for kc in ORDER:
            if t == 0:
                loads["e", kc].wait()
                loads["s", kc].wait()
            else:
                for copy in faces(t - 1, kc):
                    copy.wait_send()
            wait_around(t, kc)
            far_copy(t, kc).wait_recv()

            @pl.loop(0, nj // UNROLL)
            def _(g, now=now, before=before, kc=kc):
                for u in range(UNROLL):
                    j = 1 + g * UNROLL + u
                    for i in range(1, ni + 1):
                        before[j, i, pl.ds(T + kc * T, T), :] = stepped(now, before, j, i, kc)

            for copy in faces(t + 1, kc):
                copy.start()

    t = STEPS - 1
    now, before = (levels[t], levels[t - 1])
    inner = [near] + [i for i in range(2, ni)]

    def last_step(planes, slots, kc):
        zero = jnp.zeros((T, out.shape[3]), jnp.float32)

        def loop(g, sums):
            sums = list(sums)
            for u in range(UNROLL):
                j = 1 + g * UNROLL + u
                for n, i in enumerate(planes):
                    value = stepped(now, before, j, i, kc)
                    out[j - 1, i - 1, pl.ds(kc * T, T), :] = value
                    moved = value - GUESS
                    sums[2 * n] = sums[2 * n] + moved
                    sums[2 * n + 1] = sums[2 * n + 1] + moved * moved
            return tuple(sums)

        sums = lax.fori_loop(0, nj // UNROLL, loop, (zero,) * (2 * len(planes)))
        for n, slot in enumerate(slots):
            stats[z, slot, 0, pl.ds(kc * T, T), :] = sums[2 * n]
            stats[z, slot, 1, pl.ds(kc * T, T), :] = sums[2 * n + 1]

    def inner_stats(n):
        part = stats.at[z, pl.ds(1, ni - 1)]
        return remote(part, part, st_send.at[n, tiles], st_recv.at[n, tiles], **others[n])

    def far_stats(n, kc):
        part = stats.at[z, 0, :, pl.ds(kc * T, T), :]
        return remote(part, part, st_send.at[n, kc], st_recv.at[n, kc], **others[n])

    def finish(i, slot, kc):
        totals = stats[0, slot, 0, pl.ds(kc * T, T), :]
        squares = stats[0, slot, 1, pl.ds(kc * T, T), :]
        for other in range(1, zs):
            totals = totals + stats[other, slot, 0, pl.ds(kc * T, T), :]
            squares = squares + stats[other, slot, 1, pl.ds(kc * T, T), :]
        count = nj * zs
        shift = totals * (1.0 / count)
        variance = squares * (1.0 / count) - shift * shift
        norm[0, i - 1, pl.ds(kc * T, T), :] = GUESS + shift
        norm[1, i - 1, pl.ds(kc * T, T), :] = lax.rsqrt(variance + 0.0001)

    for kc in ORDER:
        wait_around(t, kc)
        last_step(inner, range(1, ni), kc)
    for n in range(len(others)):
        inner_stats(n).start()
    for kc in ORDER:
        far_copy(t, kc).wait_recv()
        last_step([far], [0], kc)
        for n in range(len(others)):
            far_stats(n, kc).start()
    for n in range(len(others)):
        inner_stats(n).wait_recv()
    for n, i in enumerate(inner):
        for kc in ORDER:
            finish(i, n + 1, kc)
    for kc in ORDER:
        for n in range(len(others)):
            far_stats(n, kc).wait_recv()
        finish(far, 0, kc)

    for last in (t - 1, t):
        for kc in ORDER:
            for copy in faces(last, kc):
                copy.wait_send()
    for n in range(len(others)):
        inner_stats(n).wait_send()
        for kc in ORDER:
            far_stats(n, kc).wait_send()


def write_kernel(p, norm, scaled_hbm, end_hbm, scaled, sems):
    nj, ni, nk, _ = p.shape
    pieces = sems.shape[0] - 1
    step = nj // pieces
    end = pltpu.make_async_copy(p, end_hbm, sems.at[pieces])
    end.start()

    def copy(n):
        part = pl.ds(n * step, step)
        return pltpu.make_async_copy(scaled.at[part], scaled_hbm.at[part], sems.at[n])

    for n in range(pieces):
        for i in range(ni):
            for kc in range(nk // T):
                rows = pl.ds(kc * T, T)
                mean, scale = (norm[0, i, rows, :], norm[1, i, rows, :])

                @pl.loop(n * step, (n + 1) * step, unroll=8)
                def _(j):
                    scaled[j, i, rows, :] = (p[j, i, rows, :] - mean) * scale

        copy(n).start()
    for n in range(pieces):
        copy(n).wait()
    end.wait()


def shards(pressure, earlier, speed_square):
    nj, ni, nk, members = pressure.shape
    tiles = nk // T
    zs = lax.axis_size("rows")
    whole = pl.BlockSpec(memory_space=pl.ANY)
    vmem = pl.BlockSpec(memory_space=pltpu.VMEM)
    f32 = jnp.float32
    dma = pltpu.SemaphoreType.DMA
    p, norm = pl.pallas_call(
        exchange_kernel,
        out_shape=(
            pltpu.VMEM((nj, ni, nk, members), f32),
            pltpu.VMEM((2, ni, nk, members), f32),
        ),
        in_specs=[whole] * 3,
        out_specs=(vmem, vmem),
        scratch_shapes=[
            pltpu.VMEM((nj + 2, ni + 2, nk + 2 * T, members), f32),
            pltpu.VMEM((nj + 2, ni + 2, nk + 2 * T, members), f32),
            pltpu.VMEM((nj, ni, nk, members), f32),
            pltpu.VMEM((zs, ni, 2, nk, members), f32),
            dma((3 * tiles + 2,)),
            dma((STEPS, tiles)), dma((STEPS, tiles)),
            dma((STEPS, tiles)), dma((STEPS, tiles)),
            dma((2, STEPS, tiles)), dma((2, STEPS, tiles)),
            dma((2, STEPS)), dma((2, STEPS)),
            dma((zs - 1, tiles + 1)), dma((zs - 1, tiles + 1)),
        ],
        compiler_params=pltpu.CompilerParams(
            collective_id=0, has_side_effects=True, vmem_limit_bytes=50 << 20
        ),
        name="leapfrog",
    )(pressure, earlier, speed_square)
    pieces = 8
    return pl.pallas_call(
        write_kernel,
        out_shape=(jax.ShapeDtypeStruct(p.shape, f32),) * 2,
        in_specs=[vmem, vmem],
        out_specs=(whole, whole),
        scratch_shapes=[pltpu.VMEM(p.shape, f32), dma((pieces + 1,))],
        compiler_params=pltpu.CompilerParams(vmem_limit_bytes=20 << 20),
        name="centre_and_scale",
    )(p, norm)


def solution(mesh):
    spec = P("rows", "cols", "slabs", None)
    return jax.shard_map(shards, mesh=mesh, in_specs=(spec,) * 3, out_specs=(spec,) * 2, check_vma=False)
```

profile of v0, /device:TPU:0, one launch (start us, length us, event | category | flops | bytes accessed | tf_op | source)
XLA Modules:
  0.0 88.9 jit_solution(8590995542427643674)
XLA Ops:
  0.6 82.2 %leapfrog.1 = (f32[128,4,32,128]{3,2,1,0:T(8,128)S(1)}, f32[2,4,32,128]{3,2,1,0:T(8,128)S(1)}) custom-call(f32[128,4,32,128]{3,2,1,0:T(8,128)} %p_hbm.1, f32[128,4,32,128]{3,2,1,0:T(8,128)} %e_hbm.1, f32[128,4,32,128]{3,2,1,0:T(8,128)} %s_hbm.1), custom_call_target="tpu_custom_call" | custom-call | tf_op jit(solution)/shard_map/leapfrog/pallas_call | solution.py:289
  82.9 6.0 %centre_and_scale.1 = (f32[128,4,32,128]{3,2,1,0:T(8,128)}, f32[128,4,32,128]{3,2,1,0:T(8,128)}) custom-call(f32[128,4,32,128]{3,2,1,0:T(8,128)S(1)} %get-tuple-element.4.p, f32[2,4,32,128]{3,2,1,0:T(8,128)S(1)} %get-tuple-element.5.norm), custom_call_target="tpu_custom_call" | custom-call | tf_op jit(solution)/shard_map/centre_and_scale/pallas_call | solution.py:315
where the time goes:
time: 89 us; the launch traced here: 88.9 us
  Pallas kernels  88.3 us (99%)
    pallas_call x1, Pallas kernels, shards(): pl.pallas_call(exchange_kernel, out_shape=(pltpu.VMEM((nj, ni, nk, member...  82.2 us
    pallas_call x1, Pallas kernels, shards(): pl.pallas_call(write_kernel, out_shape=(jax.ShapeDtypeStruct(p.shape, f32...  6.02 us

commit v1 on v0

--- a/solution.py
+++ b/solution.py
@@ -11,6 +11,7 @@
 MESH = pl.DeviceIdType.MESH
 T = 8
 ORDER = (3, 0, 1, 2)
+TAIL = (2, 4, 8, 8)
 GUESS = 1.0
 UNROLL = 2
 
@@ -66,13 +67,26 @@
             src_ref=src, dst_ref=dst, send_sem=send, recv_sem=recv, device_id=where, device_id_type=MESH
         )
 
-    def far_copy(t, kc):
+    def far_piece(t, kc, n, start, size):
         ref = levels[t]
+        part = pl.ds(1 + start, size)
         return remote(
-            ref.at[body, far, rows_of(kc), :],
-            ref.at[body, (ni + 1) * (1 - core), rows_of(kc), :],
-            far_send.at[t, kc], far_recv.at[t, kc], cols=far_x,
-        )
+            ref.at[part, far, rows_of(kc), :],
+            ref.at[part, (ni + 1) * (1 - core), rows_of(kc), :],
+            far_send.at[t, kc + n], far_recv.at[t, kc + n], cols=far_x,
+        )
+
+    def pieces_of(t, kc):
+        if t < STEPS - 1 or kc != ORDER[-1]:
+            return [(kc, 0, 0, nj)]
+        starts = [0]
+        for part in TAIL:
+            starts.append(starts[-1] + nj // part)
+        ids = [0] + [tiles - kc + n for n in range(len(TAIL) - 1)]
+        return [(kc, n, a0, a1 - a0) for n, a0, a1 in zip(ids, starts, starts[1:])]
+
+    def far_copies(t, kc):
+        return [far_piece(t, *piece) for piece in pieces_of(t, kc)]
 
     def near_copy(t, kc):
         ref = levels[t]
@@ -110,7 +124,7 @@
         )
 
     def faces(t, kc):
-        yield far_copy(t, kc)
+        yield from far_copies(t, kc)
         yield near_copy(t, kc)
         yield from z_copies(t, kc)
         if kc in (0, tiles - 1):
@@ -137,14 +151,15 @@
 
     barrier = pltpu.get_barrier_semaphore()
     peers = [dict(cols=far_x), dict(cols=near_x), dict(slabs=y_up), dict(slabs=y_down)]
-    others = [dict(rows=(z + d) % zs) for d in range(1, zs)]
+    others = [dict(rows=(z + d) % zs) for d in (2, 1, 3)]
     for where in peers + others:
         pl.semaphore_signal(barrier, inc=1, device_id=where, device_id_type=MESH)
     pl.semaphore_wait(barrier, len(peers) + len(others))
 
     for kc in ORDER:
         loads["far", kc].wait()
-        far_copy(0, kc).start()
+        for copy in far_copies(0, kc):
+            copy.start()
     loads["near"].wait()
     for kc in ORDER:
         near_copy(0, kc).start()
@@ -165,7 +180,8 @@
                 for copy in faces(t - 1, kc):
                     copy.wait_send()
             wait_around(t, kc)
-            far_copy(t, kc).wait_recv()
+            for copy in far_copies(t, kc):
+                copy.wait_recv()
 
             @pl.loop(0, nj // UNROLL)
             def _(g, now=now, before=before, kc=kc):
@@ -181,13 +197,11 @@
     now, before = (levels[t], levels[t - 1])
     inner = [near] + [i for i in range(2, ni)]
 
-    def last_step(planes, slots, kc):
-        zero = jnp.zeros((T, out.shape[3]), jnp.float32)
-
+    def last_step(planes, kc, start, size, sums):
         def loop(g, sums):
             sums = list(sums)
             for u in range(UNROLL):
-                j = 1 + g * UNROLL + u
+                j = 1 + start + g * UNROLL + u
                 for n, i in enumerate(planes):
                     value = stepped(now, before, j, i, kc)
                     out[j - 1, i - 1, pl.ds(kc * T, T), :] = value
@@ -196,7 +210,11 @@
                     sums[2 * n + 1] = sums[2 * n + 1] + moved * moved
             return tuple(sums)
 
-        sums = lax.fori_loop(0, nj // UNROLL, loop, (zero,) * (2 * len(planes)))
+        if sums is None:
+            sums = (jnp.zeros((T, out.shape[3]), jnp.float32),) * (2 * len(planes))
+        return lax.fori_loop(0, size // UNROLL, loop, sums)
+
+    def put_sums(slots, kc, sums):
         for n, slot in enumerate(slots):
             stats[z, slot, 0, pl.ds(kc * T, T), :] = sums[2 * n]
             stats[z, slot, 1, pl.ds(kc * T, T), :] = sums[2 * n + 1]
@@ -223,44 +241,71 @@
 
     for kc in ORDER:
         wait_around(t, kc)
-        last_step(inner, range(1, ni), kc)
+        put_sums(range(1, ni), kc, last_step(inner, kc, 0, nj, None))
     for n in range(len(others)):
         inner_stats(n).start()
     for kc in ORDER:
-        far_copy(t, kc).wait_recv()
-        last_step([far], [0], kc)
-        for n in range(len(others)):
-            far_stats(n, kc).start()
-    for n in range(len(others)):
-        inner_stats(n).wait_recv()
-    for n, i in enumerate(inner):
-        for kc in ORDER:
-            finish(i, n + 1, kc)
-    for kc in ORDER:
+        for copy in faces(t - 1, kc):
+            copy.wait_send()
+
+    def finish_far(kc):
         for n in range(len(others)):
             far_stats(n, kc).wait_recv()
         finish(far, 0, kc)
 
-    for last in (t - 1, t):
-        for kc in ORDER:
-            for copy in faces(last, kc):
-                copy.wait_send()
-    for n in range(len(others)):
-        inner_stats(n).wait_send()
-        for kc in ORDER:
-            far_stats(n, kc).wait_send()
+    for kc in ORDER:
+        sums = None
+        for piece, copy in zip(pieces_of(t, kc), far_copies(t, kc)):
+            copy.wait_recv()
+            sums = last_step([far], kc, piece[2], piece[3], sums)
+        put_sums([0], kc, sums)
+        for n in range(len(others)):
+            far_stats(n, kc).start()
+        if kc == ORDER[1]:
+            for n in range(len(others)):
+                inner_stats(n).wait_recv()
+            for n, i in enumerate(inner):
+                for tile in ORDER:
+                    finish(i, n + 1, tile)
+            for tile in ORDER:
+                near_copy(t, tile).wait_send()
+                for copy in z_copies(t, tile):
+                    copy.wait_send()
+            for tile in (0, tiles - 1):
+                y_copy(t, tile).wait_send()
+            for n in range(len(others)):
+                inner_stats(n).wait_send()
+        if kc == ORDER[2]:
+            for tile in ORDER[:2]:
+                finish_far(tile)
+                for copy in far_copies(t, tile):
+                    copy.wait_send()
+                for n in range(len(others)):
+                    far_stats(n, tile).wait_send()
+    for tile in ORDER[2:]:
+        finish_far(tile)
+    for tile in ORDER[2:]:
+        for copy in far_copies(t, tile):
+            copy.wait_send()
+        for n in range(len(others)):
+            far_stats(n, tile).wait_send()
 
 
 def write_kernel(p, norm, scaled_hbm, end_hbm, scaled, sems):
     nj, ni, nk, _ = p.shape
-    pieces = sems.shape[0] - 1
+    pieces = sems.shape[1]
     step = nj // pieces
-    end = pltpu.make_async_copy(p, end_hbm, sems.at[pieces])
-    end.start()
+
+    def end(n):
+        part = pl.ds(n * step, step)
+        return pltpu.make_async_copy(p.at[part], end_hbm.at[part], sems.at[1, n])
+
+    for n in range(pieces):
+        end(n).start()
 
     def copy(n):
         part = pl.ds(n * step, step)
-        return pltpu.make_async_copy(scaled.at[part], scaled_hbm.at[part], sems.at[n])
+        return pltpu.make_async_copy(scaled.at[part], scaled_hbm.at[part], sems.at[0, n])
 
     for n in range(pieces):
         for i in range(ni):
@@ -275,7 +320,7 @@
         copy(n).start()
     for n in range(pieces):
         copy(n).wait()
-    end.wait()
+        end(n).wait()
 
 
 def shards(pressure, earlier, speed_square):
@@ -300,7 +345,7 @@
             pltpu.VMEM((nj, ni, nk, members), f32),
             pltpu.VMEM((zs, ni, 2, nk, members), f32),
             dma((3 * tiles + 2,)),
-            dma((STEPS, tiles)), dma((STEPS, tiles)),
+            dma((STEPS, tiles + len(TAIL) - 1)), dma((STEPS, tiles + len(TAIL) - 1)),
             dma((STEPS, tiles)), dma((STEPS, tiles)),
             dma((2, STEPS, tiles)), dma((2, STEPS, tiles)),
             dma((2, STEPS)), dma((2, STEPS)),
@@ -317,7 +362,7 @@
         out_shape=(jax.ShapeDtypeStruct(p.shape, f32),) * 2,
         in_specs=[vmem, vmem],
         out_specs=(whole, whole),
-        scratch_shapes=[pltpu.VMEM(p.shape, f32), dma((pieces + 1,))],
+        scratch_shapes=[pltpu.VMEM(p.shape, f32), dma((2, pieces))],
         compiler_params=pltpu.CompilerParams(vmem_limit_bytes=20 << 20),
         name="centre_and_scale",
     )(p, norm)

time: 89 us -> 87.9 us (0.988)
  Pallas kernels: 88.3 us -> 87.2 us
    pallas_call x1, Pallas kernels: 82.2 us -> 81.2 us  [shards(): pl.pallas_call(exchange_kernel, out_shape=(pltpu.VMEM((nj, ni, nk, member...]
where the time goes in v1:
time: 87.9 us; the launch traced here: 87.8 us
  Pallas kernels  87.2 us (99%)
    pallas_call x1, Pallas kernels, shards(): pl.pallas_call(exchange_kernel, out_shape=(pltpu.VMEM((nj, ni, nk, member...  81.2 us
    pallas_call x1, Pallas kernels, shards(): pl.pallas_call(write_kernel, out_shape=(jax.ShapeDtypeStruct(p.shape, f32...  5.96 us

profile of v1, /device:TPU:0, one launch (start us, length us, event | category | flops | bytes accessed | tf_op | source)
XLA Modules:
  0.0 87.8 jit_solution(8742667139630401783)
XLA Ops:
  0.6 81.2 %leapfrog.1 = (f32[128,4,32,128]{3,2,1,0:T(8,128)S(1)}, f32[2,4,32,128]{3,2,1,0:T(8,128)S(1)}) custom-call(f32[128,4,32,128]{3,2,1,0:T(8,128)} %p_hbm.1, f32[128,4,32,128]{3,2,1,0:T(8,128)} %e_hbm.1, f32[128,4,32,128]{3,2,1,0:T(8,128)} %s_hbm.1), custom_call_target="tpu_custom_call" | custom-call | tf_op jit(solution)/shard_map/leapfrog/pallas_call | solution.py:334
  81.9 6.0 %centre_and_scale.1 = (f32[128,4,32,128]{3,2,1,0:T(8,128)}, f32[128,4,32,128]{3,2,1,0:T(8,128)}) custom-call(f32[128,4,32,128]{3,2,1,0:T(8,128)S(1)} %get-tuple-element.4.p, f32[2,4,32,128]{3,2,1,0:T(8,128)S(1)} %get-tuple-element.5.norm), custom_call_target="tpu_custom_call" | custom-call | tf_op jit(solution)/shard_map/centre_and_scale/pallas_call | solution.py:360

commit v2 on v1

--- a/solution.py
+++ b/solution.py
@@ -19,8 +19,7 @@
 def exchange_kernel(
     p_hbm, e_hbm, s_hbm, out, norm,
     a, b, s, stats,
-    load_sem, far_send, far_recv, near_send, near_recv,
-    z_send, z_recv, y_send, y_recv, st_send, st_recv,
+    load_sem, face_send, face_recv, far_recv, sums_send, sums_recv,
 ):
     nj, ni, nk, _ = out.shape
     tiles = nk // T
@@ -39,27 +38,34 @@
     def local(src, dst, n):
         return pltpu.make_async_copy(src, dst, load_sem.at[n])
 
+    def wait_for(tiles_landed, sem):
+        depth = tiles if tiles_landed % (ni * tiles) == 0 else 1
+        part = (pl.ds(0, tiles_landed // (ni * depth)), pl.ds(0, ni), pl.ds(0, depth * T))
+        pltpu.make_async_copy(p_hbm.at[part], s.at[part], sem).wait()
+
+    plane = nj * tiles
+    near_tiles, y_tiles, z_tiles = (nj, nj * ni // T, ni)
+
     def rows_of(kc):
         return pl.ds(T + kc * T, T)
 
-    loads = {}
+    loads = []
+    for kc in ORDER:
+        loads.append(local(
+            p_hbm.at[:, far - 1, pl.ds(kc * T, T), :], a.at[body, far, rows_of(kc), :], 0
+        ))
+    loads.append(local(p_hbm.at[:, near - 1], a.at[body, near, pl.ds(T, nk), :], 1))
+    loads.append(local(
+        p_hbm.at[:, pl.ds(1, ni - 2)], a.at[body, pl.ds(2, ni - 2), pl.ds(T, nk), :], 1
+    ))
     for n, kc in enumerate(ORDER):
-        loads["far", kc] = local(
-            p_hbm.at[:, far - 1, pl.ds(kc * T, T), :], a.at[body, far, rows_of(kc), :], n
-        )
-    n = tiles
-    loads["near"] = local(p_hbm.at[:, near - 1], a.at[body, near, pl.ds(T, nk), :], n)
-    loads["mid"] = local(p_hbm.at[:, pl.ds(1, ni - 2)], a.at[body, pl.ds(2, ni - 2), pl.ds(T, nk), :], n + 1)
-    n += 2
-    for kc in ORDER:
-        loads["e", kc] = local(
-            e_hbm.at[:, :, pl.ds(kc * T, T), :], b.at[body, pl.ds(1, ni), rows_of(kc), :], n
-        )
-        loads["s", kc] = local(
-            s_hbm.at[:, :, pl.ds(kc * T, T), :], s.at[:, :, pl.ds(kc * T, T), :], n + 1
-        )
-        n += 2
-    for copy in loads.values():
+        loads.append(local(
+            e_hbm.at[:, :, pl.ds(kc * T, T), :], b.at[body, pl.ds(1, ni), rows_of(kc), :], n + 2
+        ))
+        loads.append(local(
+            s_hbm.at[:, :, pl.ds(kc * T, T), :], s.at[:, :, pl.ds(kc * T, T), :], n + 2
+        ))
+    for copy in loads:
         copy.start()
 
     def remote(src, dst, send, recv, **where):
@@ -73,7 +79,7 @@
         return remote(
             ref.at[part, far, rows_of(kc), :],
             ref.at[part, (ni + 1) * (1 - core), rows_of(kc), :],
-            far_send.at[t, kc + n], far_recv.at[t, kc + n], cols=far_x,
+            face_send.at[t], far_recv.at[kc + n] if t == STEPS - 1 else face_recv.at[t, kc], cols=far_x,
         )
 
     def pieces_of(t, kc):
@@ -93,7 +99,7 @@
         return remote(
             ref.at[body, near, rows_of(kc), :],
             ref.at[body, (ni + 1) * core, rows_of(kc), :],
-            near_send.at[t, kc], near_recv.at[t, kc], cols=near_x,
+            face_send.at[t], face_recv.at[t, kc], cols=near_x,
         )
 
     def z_copies(t, kc):
@@ -102,11 +108,11 @@
         return (
             remote(
                 ref.at[nj, cells, rows_of(kc), :], ref.at[0, cells, rows_of(kc), :],
-                z_send.at[0, t, kc], z_recv.at[0, t, kc], rows=z_up,
+                face_send.at[t], face_recv.at[t, kc], rows=z_up,
             ),
             remote(
                 ref.at[1, cells, rows_of(kc), :], ref.at[nj + 1, cells, rows_of(kc), :],
-                z_send.at[1, t, kc], z_recv.at[1, t, kc], rows=z_down,
+                face_send.at[t], face_recv.at[t, kc], rows=z_down,
             ),
         )
 
@@ -116,11 +122,11 @@
         if kc == 0:
             return remote(
                 ref.at[body, cells, pl.ds(T, 1), :], ref.at[body, cells, pl.ds(T + nk, 1), :],
-                y_send.at[0, t], y_recv.at[0, t], slabs=y_down,
+                face_send.at[t], face_recv.at[t, tiles - 1], slabs=y_down,
             )
         return remote(
             ref.at[body, cells, pl.ds(T + nk - 1, 1), :], ref.at[body, cells, pl.ds(T - 1, 1), :],
-            y_send.at[1, t], y_recv.at[1, t], slabs=y_up,
+            face_send.at[t], face_recv.at[t, 0], slabs=y_up,
         )
 
     def faces(t, kc):
@@ -130,14 +136,16 @@
         if kc in (0, tiles - 1):
             yield y_copy(t, kc)
 
-    def wait_around(t, kc):
-        near_copy(t, kc).wait_recv()
-        for copy in z_copies(t, kc):
-            copy.wait_recv()
-        if kc == 0:
-            y_copy(t, tiles - 1).wait_recv()
-        if kc == tiles - 1:
-            y_copy(t, 0).wait_recv()
+    def wait_faces(t, kc):
+        landed = near_tiles + 2 * z_tiles
+        if t < STEPS - 1:
+            landed += near_tiles
+        if kc in (0, tiles - 1):
+            landed += y_tiles
+        wait_for(landed, face_recv.at[t, kc])
+
+    def wait_faces_sent(t):
+        wait_for(2 * plane + 2 * z_tiles * tiles + 2 * y_tiles, face_send.at[t])
 
     def stepped(now, before, j, i, kc):
         r = T + kc * T
@@ -156,14 +164,13 @@
         pl.semaphore_signal(barrier, inc=1, device_id=where, device_id_type=MESH)
     pl.semaphore_wait(barrier, len(peers) + len(others))
 
-    for kc in ORDER:
-        loads["far", kc].wait()
+    wait_for(plane, load_sem.at[0])
+    for kc in ORDER:
         for copy in far_copies(0, kc):
             copy.start()
-    loads["near"].wait()
+    wait_for((ni - 1) * plane, load_sem.at[1])
     for kc in ORDER:
         near_copy(0, kc).start()
-    loads["mid"].wait()
     for kc in ORDER:
         for copy in z_copies(0, kc):
             copy.start()
@@ -172,16 +179,12 @@
 
     for t in range(STEPS - 1):
         now, before = (levels[t], levels[(t + 1) % 2])
-        for kc in ORDER:
+        if t > 0:
+            wait_faces_sent(t - 1)
+        for n, kc in enumerate(ORDER):
             if t == 0:
-                loads["e", kc].wait()
-                loads["s", kc].wait()
-            else:
-                for copy in faces(t - 1, kc):
-                    copy.wait_send()
-            wait_around(t, kc)
-            for copy in far_copies(t, kc):
-                copy.wait_recv()
+                wait_for(2 * ni * nj, load_sem.at[n + 2])
+            wait_faces(t, kc)
 
             @pl.loop(0, nj // UNROLL)
             def _(g, now=now, before=before, kc=kc):
@@ -219,13 +222,9 @@
             stats[z, slot, 0, pl.ds(kc * T, T), :] = sums[2 * n]
             stats[z, slot, 1, pl.ds(kc * T, T), :] = sums[2 * n + 1]
 
-    def inner_stats(n):
-        part = stats.at[z, pl.ds(1, ni - 1)]
-        return remote(part, part, st_send.at[n, tiles], st_recv.at[n, tiles], **others[n])
-
-    def far_stats(n, kc):
-        part = stats.at[z, 0, :, pl.ds(kc * T, T), :]
-        return remote(part, part, st_send.at[n, kc], st_recv.at[n, kc], **others[n])
+    def send_sums(part, group):
+        for where in others:
+            remote(part, part, sums_send, sums_recv.at[group], **where).start()
 
     def finish(i, slot, kc):
         totals = stats[0, slot, 0, pl.ds(kc * T, T), :]
@@ -240,55 +239,30 @@
         norm[1, i - 1, pl.ds(kc * T, T), :] = lax.rsqrt(variance + 0.0001)
 
     for kc in ORDER:
-        wait_around(t, kc)
+        wait_faces(t, kc)
         put_sums(range(1, ni), kc, last_step(inner, kc, 0, nj, None))
-    for n in range(len(others)):
-        inner_stats(n).start()
-    for kc in ORDER:
-        for copy in faces(t - 1, kc):
-            copy.wait_send()
-
-    def finish_far(kc):
-        for n in range(len(others)):
-            far_stats(n, kc).wait_recv()
-        finish(far, 0, kc)
-
-    for kc in ORDER:
+    send_sums(stats.at[z, pl.ds(1, ni - 1)], 0)
+    wait_faces_sent(t - 1)
+    peers_sums = 2 * len(others)
+    for n, kc in enumerate(ORDER):
         sums = None
         for piece, copy in zip(pieces_of(t, kc), far_copies(t, kc)):
             copy.wait_recv()
             sums = last_step([far], kc, piece[2], piece[3], sums)
         put_sums([0], kc, sums)
-        for n in range(len(others)):
-            far_stats(n, kc).start()
-        if kc == ORDER[1]:
-            for n in range(len(others)):
-                inner_stats(n).wait_recv()
-            for n, i in enumerate(inner):
+        send_sums(stats.at[z, 0, :, pl.ds(kc * T, T), :], n // 2)
+        if n == 2:
+            wait_for(peers_sums * ((ni - 1) * tiles + 2), sums_recv.at[0])
+            for slot, i in enumerate(inner):
                 for tile in ORDER:
-                    finish(i, n + 1, tile)
-            for tile in ORDER:
-                near_copy(t, tile).wait_send()
-                for copy in z_copies(t, tile):
-                    copy.wait_send()
-            for tile in (0, tiles - 1):
-                y_copy(t, tile).wait_send()
-            for n in range(len(others)):
-                inner_stats(n).wait_send()
-        if kc == ORDER[2]:
+                    finish(i, slot + 1, tile)
             for tile in ORDER[:2]:
-                finish_far(tile)
-                for copy in far_copies(t, tile):
-                    copy.wait_send()
-                for n in range(len(others)):
-                    far_stats(n, tile).wait_send()
+                finish(far, 0, tile)
+    wait_for(peers_sums * 2, sums_recv.at[1])
     for tile in ORDER[2:]:
-        finish_far(tile)
-    for tile in ORDER[2:]:
-        for copy in far_copies(t, tile):
-            copy.wait_send()
-        for n in range(len(others)):
-            far_stats(n, tile).wait_send()
+        finish(far, 0, tile)
+    wait_faces_sent(t)
+    wait_for(peers_sums * ni * tiles, sums_send)
 
 
 def write_kernel(p, norm, scaled_hbm, end_hbm, scaled, sems):
@@ -344,12 +318,9 @@
             pltpu.VMEM((nj + 2, ni + 2, nk + 2 * T, members), f32),
             pltpu.VMEM((nj, ni, nk, members), f32),
             pltpu.VMEM((zs, ni, 2, nk, members), f32),
-            dma((3 * tiles + 2,)),
-            dma((STEPS, tiles + len(TAIL) - 1)), dma((STEPS, tiles + len(TAIL) - 1)),
-            dma((STEPS, tiles)), dma((STEPS, tiles)),
-            dma((2, STEPS, tiles)), dma((2, STEPS, tiles)),
-            dma((2, STEPS)), dma((2, STEPS)),
-            dma((zs - 1, tiles + 1)), dma((zs - 1, tiles + 1)),
+            dma((tiles + 2,)),
+            dma((STEPS,)), dma((STEPS, tiles)), dma((tiles + len(TAIL) - 1,)),
+            dma, dma((2,)),
         ],
         compiler_params=pltpu.CompilerParams(
             collective_id=0, has_side_effects=True, vmem_limit_bytes=50 << 20

time: 87.9 us -> 86.7 us (0.986)
  Pallas kernels: 87.2 us -> 85.9 us
    pallas_call x1, Pallas kernels: 81.2 us -> 80 us  [shards(): pl.pallas_call(exchange_kernel, out_shape=(pltpu.VMEM((nj, ni, nk, member...]
where the time goes in v2:
time: 86.7 us; the launch traced here: 86.6 us
  Pallas kernels  85.9 us (99%)
    pallas_call x1, Pallas kernels, shards(): pl.pallas_call(exchange_kernel, out_shape=(pltpu.VMEM((nj, ni, nk, member...  80 us
    pallas_call x1, Pallas kernels, shards(): pl.pallas_call(write_kernel, out_shape=(jax.ShapeDtypeStruct(p.shape, f32...  5.96 us

profile of v2, /device:TPU:0, one launch (start us, length us, event | category | flops | bytes accessed | tf_op | source)
XLA Modules:
  0.0 86.6 jit_solution(14317628082456218834)
XLA Ops:
  0.6 80.0 %leapfrog.1 = (f32[128,4,32,128]{3,2,1,0:T(8,128)S(1)}, f32[2,4,32,128]{3,2,1,0:T(8,128)S(1)}) custom-call(f32[128,4,32,128]{3,2,1,0:T(8,128)} %p_hbm.1, f32[128,4,32,128]{3,2,1,0:T(8,128)} %e_hbm.1, f32[128,4,32,128]{3,2,1,0:T(8,128)} %s_hbm.1), custom_call_target="tpu_custom_call" | custom-call | tf_op jit(solution)/shard_map/leapfrog/pallas_call | solution.py:308
  80.6 6.0 %centre_and_scale.1 = (f32[128,4,32,128]{3,2,1,0:T(8,128)}, f32[128,4,32,128]{3,2,1,0:T(8,128)}) custom-call(f32[128,4,32,128]{3,2,1,0:T(8,128)S(1)} %get-tuple-element.4.p, f32[2,4,32,128]{3,2,1,0:T(8,128)S(1)} %get-tuple-element.5.norm), custom_call_target="tpu_custom_call" | custom-call | tf_op jit(solution)/shard_map/centre_and_scale/pallas_call | solution.py:331

commit v3 on v2

--- a/solution.py
+++ b/solution.py
@@ -160,9 +160,13 @@
     barrier = pltpu.get_barrier_semaphore()
     peers = [dict(cols=far_x), dict(cols=near_x), dict(slabs=y_up), dict(slabs=y_down)]
     others = [dict(rows=(z + d) % zs) for d in (2, 1, 3)]
-    for where in peers + others:
+    first, later = (peers[:2] + others, peers[2:])
+    even = y % 2 == 0
+    for where in first:
         pl.semaphore_signal(barrier, inc=1, device_id=where, device_id_type=MESH)
-    pl.semaphore_wait(barrier, len(peers) + len(others))
+    pl.semaphore_wait(barrier, jnp.where(even, len(first), len(first) + len(later)))
+    for where in later:
+        pl.semaphore_signal(barrier, inc=1, device_id=where, device_id_type=MESH)
 
     wait_for(plane, load_sem.at[0])
     for kc in ORDER:
@@ -174,6 +178,11 @@
     for kc in ORDER:
         for copy in z_copies(0, kc):
             copy.start()
+
+    @pl.when(even)
+    def _():
+        pl.semaphore_wait(barrier, len(later))
+
     y_copy(0, tiles - 1).start()
     y_copy(0, 0).start()
 
@@ -265,21 +274,20 @@
     wait_for(peers_sums * ni * tiles, sums_send)
 
 
-def write_kernel(p, norm, scaled_hbm, end_hbm, scaled, sems):
+def write_kernel(pieces, p, norm, scaled_hbm, end_hbm, scaled, scaled_sem, end_sem):
     nj, ni, nk, _ = p.shape
-    pieces = sems.shape[1]
     step = nj // pieces
 
     def end(n):
         part = pl.ds(n * step, step)
-        return pltpu.make_async_copy(p.at[part], end_hbm.at[part], sems.at[1, n])
+        return pltpu.make_async_copy(p.at[part], end_hbm.at[part], end_sem)
 
     for n in range(pieces):
         end(n).start()
 
     def copy(n):
         part = pl.ds(n * step, step)
-        return pltpu.make_async_copy(scaled.at[part], scaled_hbm.at[part], sems.at[0, n])
+        return pltpu.make_async_copy(scaled.at[part], scaled_hbm.at[part], scaled_sem)
 
     for n in range(pieces):
         for i in range(ni):
@@ -292,9 +300,8 @@
                     scaled[j, i, rows, :] = (p[j, i, rows, :] - mean) * scale
 
         copy(n).start()
-    for n in range(pieces):
-        copy(n).wait()
-        end(n).wait()
+    pltpu.make_async_copy(p, end_hbm, end_sem).wait()
+    pltpu.make_async_copy(scaled, scaled_hbm, scaled_sem).wait()
 
 
 def shards(pressure, earlier, speed_square):
@@ -327,13 +334,12 @@
         ),
         name="leapfrog",
     )(pressure, earlier, speed_square)
-    pieces = 8
     return pl.pallas_call(
-        write_kernel,
+        functools.partial(write_kernel, 8),
         out_shape=(jax.ShapeDtypeStruct(p.shape, f32),) * 2,
         in_specs=[vmem, vmem],
         out_specs=(whole, whole),
-        scratch_shapes=[pltpu.VMEM(p.shape, f32), dma((2, pieces))],
+        scratch_shapes=[pltpu.VMEM(p.shape, f32), dma, dma],
         compiler_params=pltpu.CompilerParams(vmem_limit_bytes=20 << 20),
         name="centre_and_scale",
     )(p, norm)

time: 86.7 us -> 86.2 us (level); the launches traced: 86.6 us -> 85.2 us
  Pallas kernels: 85.9 us -> 84.5 us
    pallas_call x1, Pallas kernels: 80 us -> 78.7 us  [shards(): pl.pallas_call(exchange_kernel, out_shape=(pltpu.VMEM((nj, ni, nk, member...]
where the time goes in v3:
time: 86.2 us; the launch traced here: 85.2 us
  Pallas kernels  84.5 us (98%)
    pallas_call x1, Pallas kernels, shards(): pl.pallas_call(exchange_kernel, out_shape=(pltpu.VMEM((nj, ni, nk, member...  78.7 us
    pallas_call x1, Pallas kernels, shards(): pl.pallas_call(functools.partial(write_kernel, 8), out_shape=(jax.ShapeDt...  5.84 us

profile of v3, /device:TPU:0, one launch (start us, length us, event | category | flops | bytes accessed | tf_op | source)
XLA Modules:
  0.0 85.2 jit_solution(278674834029403630)
XLA Ops:
  0.6 78.7 %leapfrog.1 = (f32[128,4,32,128]{3,2,1,0:T(8,128)S(1)}, f32[2,4,32,128]{3,2,1,0:T(8,128)S(1)}) custom-call(f32[128,4,32,128]{3,2,1,0:T(8,128)} %p_hbm.1, f32[128,4,32,128]{3,2,1,0:T(8,128)} %e_hbm.1, f32[128,4,32,128]{3,2,1,0:T(8,128)} %s_hbm.1), custom_call_target="tpu_custom_call" | custom-call | tf_op jit(solution)/shard_map/leapfrog/pallas_call | solution.py:315
  79.3 5.8 %centre_and_scale.1 = (f32[128,4,32,128]{3,2,1,0:T(8,128)}, f32[128,4,32,128]{3,2,1,0:T(8,128)}) custom-call(f32[128,4,32,128]{3,2,1,0:T(8,128)S(1)} %get-tuple-element.4.p, f32[2,4,32,128]{3,2,1,0:T(8,128)S(1)} %get-tuple-element.5.norm), custom_call_target="tpu_custom_call" | custom-call | tf_op jit(solution)/shard_map/centre_and_scale/pallas_call | solution.py:337

commit v4 on v3

--- a/solution.py
+++ b/solution.py
@@ -12,7 +12,6 @@
 T = 8
 ORDER = (3, 0, 1, 2)
 TAIL = (2, 4, 8, 8)
-GUESS = 1.0
 UNROLL = 2
 
 
@@ -159,7 +158,7 @@
 
     barrier = pltpu.get_barrier_semaphore()
     peers = [dict(cols=far_x), dict(cols=near_x), dict(slabs=y_up), dict(slabs=y_down)]
-    others = [dict(rows=(z + d) % zs) for d in (2, 1, 3)]
+    others = [dict(rows=(z + d) % zs) for d in (1, 3, 2)]
     first, later = (peers[:2] + others, peers[2:])
     even = y % 2 == 0
     for where in first:
@@ -209,7 +208,13 @@
     now, before = (levels[t], levels[t - 1])
     inner = [near] + [i for i in range(2, ni)]
 
+    def guess(i, kc):
+        row = (1, i, pl.ds(T + kc * T, T))
+        return 2.0 * now[row] - before[row]
+
     def last_step(planes, kc, start, size, sums):
+        guesses = [guess(i, kc) for i in planes]
+
         def loop(g, sums):
             sums = list(sums)
             for u in range(UNROLL):
@@ -217,7 +222,7 @@
                 for n, i in enumerate(planes):
                     value = stepped(now, before, j, i, kc)
                     out[j - 1, i - 1, pl.ds(kc * T, T), :] = value
-                    moved = value - GUESS
+                    moved = value - guesses[n]
                     sums[2 * n] = sums[2 * n] + moved
                     sums[2 * n + 1] = sums[2 * n + 1] + moved * moved
             return tuple(sums)
@@ -226,30 +231,29 @@
             sums = (jnp.zeros((T, out.shape[3]), jnp.float32),) * (2 * len(planes))
         return lax.fori_loop(0, size // UNROLL, loop, sums)
 
-    def put_sums(slots, kc, sums):
-        for n, slot in enumerate(slots):
-            stats[z, slot, 0, pl.ds(kc * T, T), :] = sums[2 * n]
-            stats[z, slot, 1, pl.ds(kc * T, T), :] = sums[2 * n + 1]
+    def put_sums(planes, slots, kc, sums):
+        for n, (i, slot) in enumerate(zip(planes, slots)):
+            shift = sums[2 * n] * (1.0 / nj)
+            stats[z, slot, 0, pl.ds(kc * T, T), :] = guess(i, kc) + shift
+            stats[z, slot, 1, pl.ds(kc * T, T), :] = sums[2 * n + 1] - sums[2 * n] * shift
 
     def send_sums(part, group):
         for where in others:
             remote(part, part, sums_send, sums_recv.at[group], **where).start()
 
     def finish(i, slot, kc):
-        totals = stats[0, slot, 0, pl.ds(kc * T, T), :]
-        squares = stats[0, slot, 1, pl.ds(kc * T, T), :]
-        for other in range(1, zs):
-            totals = totals + stats[other, slot, 0, pl.ds(kc * T, T), :]
-            squares = squares + stats[other, slot, 1, pl.ds(kc * T, T), :]
-        count = nj * zs
-        shift = totals * (1.0 / count)
-        variance = squares * (1.0 / count) - shift * shift
-        norm[0, i - 1, pl.ds(kc * T, T), :] = GUESS + shift
+        means = [stats[other, slot, 0, pl.ds(kc * T, T), :] for other in range(zs)]
+        squares = [stats[other, slot, 1, pl.ds(kc * T, T), :] for other in range(zs)]
+        mean = sum(means[1:], means[0]) * (1.0 / zs)
+        between = [(m - mean) * (m - mean) for m in means]
+        variance = sum(squares[1:], squares[0]) * (1.0 / (nj * zs))
+        variance = variance + sum(between[1:], between[0]) * (1.0 / zs)
+        norm[0, i - 1, pl.ds(kc * T, T), :] = mean
         norm[1, i - 1, pl.ds(kc * T, T), :] = lax.rsqrt(variance + 0.0001)
 
     for kc in ORDER:
         wait_faces(t, kc)
-        put_sums(range(1, ni), kc, last_step(inner, kc, 0, nj, None))
+        put_sums(inner, range(1, ni), kc, last_step(inner, kc, 0, nj, None))
     send_sums(stats.at[z, pl.ds(1, ni - 1)], 0)
     wait_faces_sent(t - 1)
     peers_sums = 2 * len(others)
@@ -258,7 +262,7 @@
         for piece, copy in zip(pieces_of(t, kc), far_copies(t, kc)):
             copy.wait_recv()
             sums = last_step([far], kc, piece[2], piece[3], sums)
-        put_sums([0], kc, sums)
+        put_sums([far], [0], kc, sums)
         send_sums(stats.at[z, 0, :, pl.ds(kc * T, T), :], n // 2)
         if n == 2:
             wait_for(peers_sums * ((ni - 1) * tiles + 2), sums_recv.at[0])
@@ -290,14 +294,11 @@
         return pltpu.make_async_copy(scaled.at[part], scaled_hbm.at[part], scaled_sem)
 
     for n in range(pieces):
-        for i in range(ni):
-            for kc in range(nk // T):
-                rows = pl.ds(kc * T, T)
-                mean, scale = (norm[0, i, rows, :], norm[1, i, rows, :])
-
-                @pl.loop(n * step, (n + 1) * step, unroll=8)
-                def _(j):
-                    scaled[j, i, rows, :] = (p[j, i, rows, :] - mean) * scale
+
+        @pl.loop(n * step, (n + 1) * step, unroll=2)
+        def _(j):
+            for i in range(ni):
+                scaled[j, i] = (p[j, i] - norm[0, i]) * norm[1, i]
 
         copy(n).start()
     pltpu.make_async_copy(p, end_hbm, end_sem).wait()

time: 86.2 us -> 86.3 us (level)
  no operation moved by 1% of the time
where the time goes in v4:
time: 86.3 us; the launch traced here: 85.2 us
  Pallas kernels  84.6 us (98%)
    pallas_call x1, Pallas kernels, shards(): pl.pallas_call(exchange_kernel, out_shape=(pltpu.VMEM((nj, ni, nk, member...  78.7 us
    pallas_call x1, Pallas kernels, shards(): pl.pallas_call(functools.partial(write_kernel, 8), out_shape=(jax.ShapeDt...  5.84 us

profile of v4, /device:TPU:0, one launch (start us, length us, event | category | flops | bytes accessed | tf_op | source)
XLA Modules:
  0.0 85.2 jit_solution(14800033206680249977)
XLA Ops:
  0.6 78.7 %leapfrog.1 = (f32[128,4,32,128]{3,2,1,0:T(8,128)S(1)}, f32[2,4,32,128]{3,2,1,0:T(8,128)S(1)}) custom-call(f32[128,4,32,128]{3,2,1,0:T(8,128)} %p_hbm.1, f32[128,4,32,128]{3,2,1,0:T(8,128)} %e_hbm.1, f32[128,4,32,128]{3,2,1,0:T(8,128)} %s_hbm.1), custom_call_target="tpu_custom_call" | custom-call | tf_op jit(solution)/shard_map/leapfrog/pallas_call | solution.py:316
  79.4 5.8 %centre_and_scale.1 = (f32[128,4,32,128]{3,2,1,0:T(8,128)}, f32[128,4,32,128]{3,2,1,0:T(8,128)}) custom-call(f32[128,4,32,128]{3,2,1,0:T(8,128)S(1)} %get-tuple-element.4.p, f32[2,4,32,128]{3,2,1,0:T(8,128)S(1)} %get-tuple-element.5.norm), custom_call_target="tpu_custom_call" | custom-call | tf_op jit(solution)/shard_map/centre_and_scale/pallas_call | solution.py:338

commit v5 on v4

--- a/solution.py
+++ b/solution.py
@@ -59,10 +59,10 @@
     ))
     for n, kc in enumerate(ORDER):
         loads.append(local(
-            e_hbm.at[:, :, pl.ds(kc * T, T), :], b.at[body, pl.ds(1, ni), rows_of(kc), :], n + 2
+            e_hbm.at[:, :, pl.ds(kc * T, T), :], b.at[body, pl.ds(1, ni), rows_of(kc), :], n // 2 + 2
         ))
         loads.append(local(
-            s_hbm.at[:, :, pl.ds(kc * T, T), :], s.at[:, :, pl.ds(kc * T, T), :], n + 2
+            s_hbm.at[:, :, pl.ds(kc * T, T), :], s.at[:, :, pl.ds(kc * T, T), :], n // 2 + 2
         ))
     for copy in loads:
         copy.start()
@@ -78,7 +78,7 @@
         return remote(
             ref.at[part, far, rows_of(kc), :],
             ref.at[part, (ni + 1) * (1 - core), rows_of(kc), :],
-            face_send.at[t], far_recv.at[kc + n] if t == STEPS - 1 else face_recv.at[t, kc], cols=far_x,
+            face_send.at[t % 2], far_recv.at[kc + n] if t == STEPS - 1 else face_recv.at[t % 2, kc], cols=far_x,
         )
 
     def pieces_of(t, kc):
@@ -98,7 +98,7 @@
         return remote(
             ref.at[body, near, rows_of(kc), :],
             ref.at[body, (ni + 1) * core, rows_of(kc), :],
-            face_send.at[t], face_recv.at[t, kc], cols=near_x,
+            face_send.at[t % 2], face_recv.at[t % 2, kc], cols=near_x,
         )
 
     def z_copies(t, kc):
@@ -107,11 +107,11 @@
         return (
             remote(
                 ref.at[nj, cells, rows_of(kc), :], ref.at[0, cells, rows_of(kc), :],
-                face_send.at[t], face_recv.at[t, kc], rows=z_up,
+                face_send.at[t % 2], face_recv.at[t % 2, kc], rows=z_up,
             ),
             remote(
                 ref.at[1, cells, rows_of(kc), :], ref.at[nj + 1, cells, rows_of(kc), :],
-                face_send.at[t], face_recv.at[t, kc], rows=z_down,
+                face_send.at[t % 2], face_recv.at[t % 2, kc], rows=z_down,
             ),
         )
 
@@ -121,11 +121,11 @@
         if kc == 0:
             return remote(
                 ref.at[body, cells, pl.ds(T, 1), :], ref.at[body, cells, pl.ds(T + nk, 1), :],
-                face_send.at[t], face_recv.at[t, tiles - 1], slabs=y_down,
+                face_send.at[t % 2], face_recv.at[t % 2, tiles - 1], slabs=y_down,
             )
         return remote(
             ref.at[body, cells, pl.ds(T + nk - 1, 1), :], ref.at[body, cells, pl.ds(T - 1, 1), :],
-            face_send.at[t], face_recv.at[t, 0], slabs=y_up,
+            face_send.at[t % 2], face_recv.at[t % 2, 0], slabs=y_up,
         )
 
     def faces(t, kc):
@@ -141,10 +141,10 @@
             landed += near_tiles
         if kc in (0, tiles - 1):
             landed += y_tiles
-        wait_for(landed, face_recv.at[t, kc])
+        wait_for(landed, face_recv.at[t % 2, kc])
 
     def wait_faces_sent(t):
-        wait_for(2 * plane + 2 * z_tiles * tiles + 2 * y_tiles, face_send.at[t])
+        wait_for(2 * plane + 2 * z_tiles * tiles + 2 * y_tiles, face_send.at[t % 2])
 
     def stepped(now, before, j, i, kc):
         r = T + kc * T
@@ -190,8 +190,8 @@
         if t > 0:
             wait_faces_sent(t - 1)
         for n, kc in enumerate(ORDER):
-            if t == 0:
-                wait_for(2 * ni * nj, load_sem.at[n + 2])
+            if t == 0 and n % 2 == 0:
+                wait_for(4 * ni * nj, load_sem.at[n // 2 + 2])
             wait_faces(t, kc)
 
             @pl.loop(0, nj // UNROLL)
@@ -326,8 +326,8 @@
             pltpu.VMEM((nj + 2, ni + 2, nk + 2 * T, members), f32),
             pltpu.VMEM((nj, ni, nk, members), f32),
             pltpu.VMEM((zs, ni, 2, nk, members), f32),
-            dma((tiles + 2,)),
-            dma((STEPS,)), dma((STEPS, tiles)), dma((tiles + len(TAIL) - 1,)),
+            dma((tiles // 2 + 2,)),
+            dma((2,)), dma((2, tiles)), dma((tiles + len(TAIL) - 1,)),
             dma, dma((2,)),
         ],
         compiler_params=pltpu.CompilerParams(

time: 86.3 us -> 86.2 us (level)
  no operation moved by 1% of the time
where the time goes in v5:
time: 86.2 us; the launch traced here: 85.1 us
  Pallas kernels  84.5 us (98%)
    pallas_call x1, Pallas kernels, shards(): pl.pallas_call(exchange_kernel, out_shape=(pltpu.VMEM((nj, ni, nk, member...  78.7 us
    pallas_call x1, Pallas kernels, shards(): pl.pallas_call(functools.partial(write_kernel, 8), out_shape=(jax.ShapeDt...  5.84 us

profile of v5, /device:TPU:0, one launch (start us, length us, event | category | flops | bytes accessed | tf_op | source)
XLA Modules:
  0.0 85.1 jit_solution(12002392359400677684)
XLA Ops:
  0.6 78.7 %leapfrog.1 = (f32[128,4,32,128]{3,2,1,0:T(8,128)S(1)}, f32[2,4,32,128]{3,2,1,0:T(8,128)S(1)}) custom-call(f32[128,4,32,128]{3,2,1,0:T(8,128)} %p_hbm.1, f32[128,4,32,128]{3,2,1,0:T(8,128)} %e_hbm.1, f32[128,4,32,128]{3,2,1,0:T(8,128)} %s_hbm.1), custom_call_target="tpu_custom_call" | custom-call | tf_op jit(solution)/shard_map/leapfrog/pallas_call | solution.py:316
  79.3 5.8 %centre_and_scale.1 = (f32[128,4,32,128]{3,2,1,0:T(8,128)}, f32[128,4,32,128]{3,2,1,0:T(8,128)}) custom-call(f32[128,4,32,128]{3,2,1,0:T(8,128)S(1)} %get-tuple-element.4.p, f32[2,4,32,128]{3,2,1,0:T(8,128)S(1)} %get-tuple-element.5.norm), custom_call_target="tpu_custom_call" | custom-call | tf_op jit(solution)/shard_map/centre_and_scale/pallas_call | solution.py:338
